TPU v7x, 32 devices: a whole 2x2x4 slice. The times are simulated.
32 devices in a mesh: gx: 4 (over x, core), gy: 4 (over z), gz: 2 (over y).
Axes of the slice: x: 2, y: 2, z: 4, core: 2. Of those that a mesh axis runs over, the one named last changes fastest.
Arguments:
- particle_fields: float32 [20, 262144], P(None, ('gx', 'gy', 'gz')), may hold values from -4 to 4
- step_length: float32 [262144], P(('gx', 'gy', 'gz')), may hold values from 0.1 to 1
- live_mask: int32 [262144], P(('gx', 'gy', 'gz')), may hold values 0 or 1
- dest_cell: int32 [262144], P(('gx', 'gy', 'gz')), may hold values from 0 to 511
- block_counts: int32 [32, 6], P(('gx', 'gy', 'gz')), may hold values from 0 to 12, as said below
- block_lists: int32 [32, 48], P(('gx', 'gy', 'gz')), may hold values from 0 to 87, as said below
Outputs:
- tile_sums: float32 [20, 16384], P(None, ('gx', 'gy', 'gz'))
Inputs may be any that keep to these rules, and one draw needn't show every extreme that they name: `block_counts`: columns are directions in the order x lower, x upper, z lower, z upper, y lower, y upper; a count is at most its section's span (6, 6 or 12) and may be 0; at every section some domain receives full spans from both neighbours. `block_lists`: per domain, 6 entries toward the lower x neighbour, 6 toward the upper, then 2 * 6 for z and 24 for y in the same way; entries are block numbers of the domain's pool at that section. Entries below their direction's count are valid: valid entries of one domain over all sections are distinct, and each names an own block or an appended block that its sender filled. Other entries are arbitrary numbers within the pool.
All inputs are finite; a program needn't handle non-finite values. No bound on the sum of `live_mask` on one device may be relied on, other than what follows from the above.
Results may differ from a plain program's by a relative error of at most 0.0003.
Values sent between devices are 32-bit elements; how exact they have to be, the bound alone decides.
A program may use at most 64 MiB of HBM per device.

v0:
```python
import jax
import jax.numpy as jnp
from jax import lax
from jax.sharding import PartitionSpec as P

CELLS = 512
CAP_X = 6
CAP_Z = 6
CAP_Y = 12


def padded_2(array, sides, width):
    for axis, dim in sides:
        devices, length = (lax.axis_size(axis), array.shape[dim])
        up = [(i, (i + 1) % devices) for i in range(devices)]
        down = [(j, i) for i, j in up]
        last = lax.slice_in_dim(array, length - width, length, axis=dim)
        initial = lax.slice_in_dim(array, 0, width, axis=dim)
        before = lax.ppermute(last, axis, up)
        after = lax.ppermute(initial, axis, down)
        array = jnp.concatenate([before, array, after], axis=dim)
    return array


def pick_blocks(holding, chosen, toward_lower, toward_upper):
    extent = chosen.shape[0] // 2
    picked = jnp.take(holding, chosen, axis=1)
    position = jnp.arange(2 * extent) % extent
    wanted = jnp.where(jnp.arange(2 * extent) < extent, toward_lower, toward_upper)
    usable = (position < wanted).astype(jnp.float32)
    return picked * usable[None, :, None]


def arrived(padded, extent):
    margin = extent * 128
    lower_part = padded[:, :margin]
    upper_part = padded[:, padded.shape[1] - margin :]
    return jnp.concatenate([lower_part, upper_part], axis=1).reshape(
        padded.shape[0], 2 * extent, 128
    )


def group_width(block_total):
    for stride in (16, 8, 4, 2):
        if block_total % stride == 0:
            return stride
    return 1


def bin_blocks(holding, weights, tile_count):
    row_count, block_count, lane_count = holding.shape
    field_count = row_count - 2
    stride = group_width(block_count) * lane_count
    weighted = (holding[:field_count] * weights[None]).reshape(
        field_count, block_count * lane_count
    )
    cell_row = holding[row_count - 1].reshape(block_count * lane_count)
    tile_values = jnp.arange(tile_count, dtype=jnp.float32)

    def add_group(counter, running):
        offset = counter * stride
        portion = lax.dynamic_slice_in_dim(weighted, offset, stride, 1)
        cell_slice = lax.dynamic_slice_in_dim(cell_row, offset, stride, 0)
        one_hot = (cell_slice[:, None] == tile_values[None, :]).astype(jnp.float32)
        return running + jnp.dot(
            portion, one_hot, precision=lax.Precision.HIGHEST, preferred_element_type=jnp.float32
        )

    return lax.fori_loop(
        0,
        block_count * lane_count // stride,
        add_group,
        jnp.zeros((field_count, tile_count), jnp.float32),
    )


def per_device(particle_fields, step_length, live_mask, dest_cell, block_counts, block_lists):
    field_count = particle_fields.shape[0]
    row_count = field_count + 2
    advanced = particle_fields[0:3] + step_length[None, :] * particle_fields[3:6]
    carried = jnp.concatenate(
        [
            advanced,
            particle_fields[3:],
            live_mask.astype(jnp.float32)[None, :],
            dest_cell.astype(jnp.float32)[None, :],
        ],
        axis=0,
    )
    blocks_held = carried.reshape(row_count, -1, 128)
    number = block_counts[0]
    entries = block_lists[0]
    first_end = 2 * CAP_X
    second_end = first_end + 2 * CAP_Z
    outgoing = pick_blocks(blocks_held, entries[:first_end], number[0], number[1])
    padded = padded_2(outgoing.reshape(row_count, -1), (("gx", 1),), CAP_X * 128)
    blocks_held = jnp.concatenate([blocks_held, arrived(padded, CAP_X)], axis=1)
    outgoing = pick_blocks(blocks_held, entries[first_end:second_end], number[2], number[3])
    padded = padded_2(outgoing.reshape(row_count, -1), (("gz", 1),), CAP_Z * 128)
    blocks_held = jnp.concatenate([blocks_held, arrived(padded, CAP_Z)], axis=1)
    outgoing = pick_blocks(blocks_held, entries[second_end:], number[4], number[5])
    block_index = jnp.arange(blocks_held.shape[1])
    limits = []
    for section_index, extent in enumerate((CAP_X, CAP_Z, CAP_Y)):
        for side_index in range(2):
            limits.append(jnp.broadcast_to(number[2 * section_index + side_index], (extent,)))
    wanted = jnp.concatenate(limits)
    position = jnp.concatenate(
        [jnp.arange(extent) for extent in (CAP_X, CAP_X, CAP_Z, CAP_Z, CAP_Y, CAP_Y)]
    )
    listed = (entries[:, None] == block_index[None, :]) & (position < wanted)[:, None]
    keep_block = 1.0 - jnp.any(listed, axis=0).astype(jnp.float32)
    weights = blocks_held[field_count] * keep_block[:, None]
    padded = padded_2(outgoing.reshape(row_count, -1), (("gy", 1),), CAP_Y * 128)
    landed = arrived(padded, CAP_Y)
    tile_sums = bin_blocks(blocks_held, weights, CELLS) + bin_blocks(
        landed, landed[field_count], CELLS
    )
    return tile_sums


def solution(mesh):
    placed = (
        P(None, ("gx", "gy", "gz")),
        P(("gx", "gy", "gz")),
        P(("gx", "gy", "gz")),
        P(("gx", "gy", "gz")),
        P(("gx", "gy", "gz"), None),
        P(("gx", "gy", "gz"), None),
    )
    return jax.shard_map(
        per_device,
        mesh=mesh,
        in_specs=placed,
        out_specs=P(None, ("gx", "gy", "gz")),
        check_vma=False,
    )
```

profile of v0, /device:TPU:0, one launch (start us, length us, event | category | flops | bytes accessed | tf_op | source)
XLA Modules:
  0.0 44.3 jit_solution(10634139163812123180)
XLA Ops:
  0.0 0.8 %fusion.17 = (s32[12]{0:T(128)S(1)}, s32[12]{0:T(128)S(1)}) fusion(s32[1,48]{1,0:T(1,128)} %param.15), kind=kLoop, calls=%fused_computation.61 | loop fusion | flops 72 | bytes 192 | tf_op jit(solution)/shard_map/jit(_take)/jit(_where)/select_n | solution.py:27
  0.8 0.8 %compare_and_fusion.1 = (pred[12]{0:T(512)(128)(4,1)S(1)}, pred[12]{0:T(512)(128)(4,1)S(1)}) fusion(s32[1,48]{1,0:T(1,128)} %param.15), kind=kLoop, calls=%fused_computation.54 | loop fusion | flops 144 | bytes 120 | tf_op jit(solution)/shard_map/jit(_take)/and | solution.py:27
  1.6 1.5 %fusion.24 = (s32[1,1]{1,0:T(1,128)}, s32[1,1]{1,0:T(1,128)}, s32[1,1]{1,0:T(1,128)}, s32[1,1]{1,0:T(1,128)}, s32[1,1]{1,0:T(1,128)}, /*index=5*/s32[1,1]{1,0:T(1,128)}) fusion(s32[1,6]{1,0:T(1,128)} %param.14), kind=kLoop, calls=%fused_computation.69 | loop fusion | bytes 48 | tf_op jit(solution)/shard_map/slice | solution.py:106
  3.2 1.3 %compare_convert_fusion.2 = f32[12]{0:T(128)S(1)} fusion(s32[]{:T(128)} %bitcast.9, s32[]{:T(128)} %bitcast.8), kind=kLoop, calls=%fused_computation.55 | loop fusion | flops 120 | bytes 56 | tf_op jit(solution)/shard_map/convert_element_type | solution.py:30
  4.5 1.2 %slice.104 = f32[17,8192]{1,0:T(8,128)S(1)} slice(f32[20,8192]{1,0:T(8,128)} %param.10), slice={[3:20], [0:8192]} | slice | bytes 1114112 | tf_op jit(solution)/shard_map/slice | solution.py:84
  6.6 1.1 %add_bitcast_fusion = f32[3,64,128]{2,0,1:T(4,128)S(1)} fusion(f32[20,8192]{1,0:T(8,128)} %param.10, f32[8192]{0:T(1024)S(1)} %copy-done.2), kind=kLoop, calls=%fused_computation.27 | loop fusion | flops 49152 | bytes 327680 | tf_op jit(solution)/shard_map/concatenate | solution.py:81
  9.3 2.0 %collective-permute-start.1 = (f32[22,768]{1,0:T(8,128)S(1)}, f32[22,768]{1,0:T(8,128)S(1)}, u32[]{:S(2)}, u32[]{:S(2)}) collective-permute-start(f32[22,768]{1,0:T(8,128)S(1)} %get-tuple-element.254), channel_id=1, source_target_pairs={{8,0},{16,8},{24,16},{0,24},{9,1},{17,9},{25,17},{1,25},{10,2},{18... | collective-permute-start | bytes 202760 | tf_op jit(solution)/shard_map/ppermute | solution.py:20
  11.4 1.3 %compare_convert_fusion.1 = f32[12]{0:T(128)S(1)} fusion(s32[]{:T(128)} %bitcast.17, s32[]{:T(128)} %bitcast.16), kind=kLoop, calls=%fused_computation.53 | loop fusion | flops 120 | bytes 56 | tf_op jit(solution)/shard_map/convert_element_type | solution.py:30
  12.7 1.3 %compare_convert_fusion = f32[24]{0:T(128)S(1)} fusion(s32[]{:T(128)} %bitcast.21, s32[]{:T(128)} %bitcast.20), kind=kLoop, calls=%fused_computation.49 | loop fusion | flops 240 | bytes 104 | tf_op jit(solution)/shard_map/convert_element_type | solution.py:30
  19.3 2.3 %collective-permute-start.2 = (f32[22,768]{1,0:T(8,128)S(1)}, f32[22,768]{1,0:T(8,128)S(1)}, u32[]{:S(2)}, u32[]{:S(2)}) collective-permute-start(f32[22,768]{1,0:T(8,128)S(1)} %get-tuple-element.251), channel_id=1, source_target_pairs={{0,1},{1,0},{2,3},{3,2},{4,5},{5,4},{6,7},{7,6},{8,9},{9,8},{10,11... | collective-permute-start | bytes 202760 | tf_op jit(solution)/shard_map/ppermute | solution.py:19
  21.8 2.8 %collective-permute-done.2 = f32[22,768]{1,0:T(8,128)S(1)} collective-permute-done((f32[22,768]{1,0:T(8,128)S(1)}, f32[22,768]{1,0:T(8,128)S(1)}, u32[]{:S(2)}, u32[]{:S(2)}) %collective-permute-start.2) | collective-permute-done | bytes 67616 | tf_op jit(solution)/shard_map/ppermute | solution.py:19
  24.5 1.5 %collective-permute-done.3 = f32[22,768]{1,0:T(8,128)S(1)} collective-permute-done((f32[22,768]{1,0:T(8,128)S(1)}, f32[22,768]{1,0:T(8,128)S(1)}, u32[]{:S(2)}, u32[]{:S(2)}) %collective-permute-start.3) | collective-permute-done | bytes 67616 | tf_op jit(solution)/shard_map/ppermute | solution.py:20
  27.1 1.7 %collective-permute-start.4 = (f32[22,1536]{1,0:T(8,128)S(1)}, f32[22,1536]{1,0:T(8,128)S(1)}, u32[]{:S(2)}, u32[]{:S(2)}) collective-permute-start(f32[22,1536]{1,0:T(8,128)S(1)} %get-tuple-element.250), channel_id=1, source_target_pairs={{0,2},{2,4},{4,6},{6,0},{1,3},{3,5},{5,7},{7,1},{8,10},{10,12},{12... | collective-permute-start | bytes 405512 | tf_op jit(solution)/shard_map/ppermute | solution.py:19
  28.8 2.2 %collective-permute-start.5 = (f32[22,1536]{1,0:T(8,128)S(1)}, f32[22,1536]{1,0:T(8,128)S(1)}, u32[]{:S(2)}, u32[]{:S(2)}) collective-permute-start(f32[22,1536]{1,0:T(8,128)S(1)} %get-tuple-element.249), channel_id=1, source_target_pairs={{2,0},{4,2},{6,4},{0,6},{3,1},{5,3},{7,5},{1,7},{10,8},{12,10},{14... | collective-permute-start | bytes 405512 | tf_op jit(solution)/shard_map/ppermute | solution.py:20
  31.8 9.3 %while.28 = (s32[]{:T(128)}, f32[20,512]{1,0:T(8,128)S(1)}, f32[20,11264]{1,0:T(8,128)S(1)}, f32[11264]{0:T(1024)S(1)}, s32[]{:T(128)}, /*index=5*/s32[]{:T(128)}, s32[]{:T(128)}, s32[]{:T(128)}) while((s32[]{:T(128)}, f32[20,512]{1,0:T(8,128)S(1)}, f32[20,11264]{1,0:T(8,128)S(1)}, f32[11264]{0:T(1024)S(1)}, s32[]{:T(128)}, ...), condition=%wide.region_2.3_spmd.clone, body=%wide.region_1.2_spmd.clone.sunk | while | flops 126373896 | bytes 200853 | solution.py:69
  31.8 0.8 %fusion.30 = f32[20,512]{1,0:T(8,128)S(1)} fusion(f32[1024]{0:T(1024)S(1)} %dynamic_slice.41, f32[20,11264]{1,0:T(8,128)S(1)} %get-tuple-element.337, s32[]{:T(128)S(6)} %select_n.185, f32[20,512]{1,0:T(8,128)S(1)} %get-tuple-element.328, pred[]{:T(512)S(6)} %compare.6), kind=kOutput, calls=%fused_computation.7.clone.1 | convolution fusion | flops 126373888 | bytes 192517 | tf_op jit(solution)/shard_map/while/body/eval_jaxpr/dot_general | solution.py:65
  32.6 0.8 %fusion.30 = f32[20,512]{1,0:T(8,128)S(1)} fusion(f32[1024]{0:T(1024)S(1)} %dynamic_slice.41, f32[20,11264]{1,0:T(8,128)S(1)} %get-tuple-element.337, s32[]{:T(128)S(6)} %select_n.185, f32[20,512]{1,0:T(8,128)S(1)} %get-tuple-element.328, pred[]{:T(512)S(6)} %compare.6), kind=kOutput, calls=%fused_computation.7.clone.1 | convolution fusion | flops 126373888 | bytes 192517 | tf_op jit(solution)/shard_map/while/body/eval_jaxpr/dot_general | solution.py:65
  33.5 0.8 %fusion.30 = f32[20,512]{1,0:T(8,128)S(1)} fusion(f32[1024]{0:T(1024)S(1)} %dynamic_slice.41, f32[20,11264]{1,0:T(8,128)S(1)} %get-tuple-element.337, s32[]{:T(128)S(6)} %select_n.185, f32[20,512]{1,0:T(8,128)S(1)} %get-tuple-element.328, pred[]{:T(512)S(6)} %compare.6), kind=kOutput, calls=%fused_computation.7.clone.1 | convolution fusion | flops 126373888 | bytes 192517 | tf_op jit(solution)/shard_map/while/body/eval_jaxpr/dot_general | solution.py:65
  34.3 0.8 %fusion.30 = f32[20,512]{1,0:T(8,128)S(1)} fusion(f32[1024]{0:T(1024)S(1)} %dynamic_slice.41, f32[20,11264]{1,0:T(8,128)S(1)} %get-tuple-element.337, s32[]{:T(128)S(6)} %select_n.185, f32[20,512]{1,0:T(8,128)S(1)} %get-tuple-element.328, pred[]{:T(512)S(6)} %compare.6), kind=kOutput, calls=%fused_computation.7.clone.1 | convolution fusion | flops 126373888 | bytes 192517 | tf_op jit(solution)/shard_map/while/body/eval_jaxpr/dot_general | solution.py:65
  35.2 0.8 %fusion.30 = f32[20,512]{1,0:T(8,128)S(1)} fusion(f32[1024]{0:T(1024)S(1)} %dynamic_slice.41, f32[20,11264]{1,0:T(8,128)S(1)} %get-tuple-element.337, s32[]{:T(128)S(6)} %select_n.185, f32[20,512]{1,0:T(8,128)S(1)} %get-tuple-element.328, pred[]{:T(512)S(6)} %compare.6), kind=kOutput, calls=%fused_computation.7.clone.1 | convolution fusion | flops 126373888 | bytes 192517 | tf_op jit(solution)/shard_map/while/body/eval_jaxpr/dot_general | solution.py:65
  38.5 0.8 %fusion.30 = f32[20,512]{1,0:T(8,128)S(1)} fusion(f32[1024]{0:T(1024)S(1)} %dynamic_slice.41, f32[20,11264]{1,0:T(8,128)S(1)} %get-tuple-element.337, s32[]{:T(128)S(6)} %select_n.185, f32[20,512]{1,0:T(8,128)S(1)} %get-tuple-element.328, pred[]{:T(512)S(6)} %compare.6), kind=kOutput, calls=%fused_computation.7.clone.1 | convolution fusion | flops 126373888 | bytes 192517 | tf_op jit(solution)/shard_map/while/body/eval_jaxpr/dot_general | solution.py:65
  39.4 0.8 %fusion.30 = f32[20,512]{1,0:T(8,128)S(1)} fusion(f32[1024]{0:T(1024)S(1)} %dynamic_slice.41, f32[20,11264]{1,0:T(8,128)S(1)} %get-tuple-element.337, s32[]{:T(128)S(6)} %select_n.185, f32[20,512]{1,0:T(8,128)S(1)} %get-tuple-element.328, pred[]{:T(512)S(6)} %compare.6), kind=kOutput, calls=%fused_computation.7.clone.1 | convolution fusion | flops 126373888 | bytes 192517 | tf_op jit(solution)/shard_map/while/body/eval_jaxpr/dot_general | solution.py:65
  40.2 0.8 %fusion.30 = f32[20,512]{1,0:T(8,128)S(1)} fusion(f32[1024]{0:T(1024)S(1)} %dynamic_slice.41, f32[20,11264]{1,0:T(8,128)S(1)} %get-tuple-element.337, s32[]{:T(128)S(6)} %select_n.185, f32[20,512]{1,0:T(8,128)S(1)} %get-tuple-element.328, pred[]{:T(512)S(6)} %compare.6), kind=kOutput, calls=%fused_computation.7.clone.1 | convolution fusion | flops 126373888 | bytes 192517 | tf_op jit(solution)/shard_map/while/body/eval_jaxpr/dot_general | solution.py:65
  41.1 2.5 %while.29 = (s32[]{:T(128)}, f32[20,512]{1,0:T(8,128)S(1)}, f32[20,3072]{1,0:T(8,128)S(1)}, f32[3072]{0:T(1024)S(1)}, s32[]{:T(128)}, /*index=5*/s32[]{:T(128)}, s32[]{:T(128)}, s32[]{:T(128)}) while((s32[]{:T(128)}, f32[20,512]{1,0:T(8,128)S(1)}, f32[20,3072]{1,0:T(8,128)S(1)}, f32[3072]{0:T(1024)S(1)}, s32[]{:T(128)}, ...), condition=%wide.region_4.5_spmd.clone, body=%wide.region_3.4_spmd.clone.sunk | while | flops 126373896 | bytes 200853 | solution.py:69
  (100 shorter events, 15.2 us)
Async XLA Ops:
  5.8 0.8 %copy-start.2 = (f32[8192]{0:T(1024)S(1)}, f32[8192]{0:T(1024)}, u32[]{:S(2)}) copy-start(f32[8192]{0:T(1024)} %param.11) | copy-start | bytes 98308
  5.9 1.8 %copy-start = (s32[8192]{0:T(1024)S(1)}, s32[8192]{0:T(1024)}, u32[]{:S(2)}) copy-start(s32[8192]{0:T(1024)} %param.12) | copy-start | bytes 98308
  5.9 1.8 %copy-start.1 = (s32[8192]{0:T(1024)S(1)}, s32[8192]{0:T(1024)}, u32[]{:S(2)}) copy-start(s32[8192]{0:T(1024)} %param.13) | copy-start | bytes 98308
  7.9 3.3 %copy-start.3 = (s32[1,48]{1,0:T(1,128)S(1)}, s32[1,48]{1,0:T(1,128)}, u32[]{:S(2)}) copy-start(s32[1,48]{1,0:T(1,128)} %param.15) | copy-start | bytes 580
  8.7 9.6 %collective-permute-start = (f32[22,768]{1,0:T(8,128)S(1)}, f32[22,768]{1,0:T(8,128)S(1)}, u32[]{:S(2)}, u32[]{:S(2)}) collective-permute-start(f32[22,768]{1,0:T(8,128)S(1)} %get-tuple-element.253), channel_id=1, source_target_pairs={{0,8},{8,16},{16,24},{24,0},{1,9},{9,17},{17,25},{25,1},{2,10},{10... | collective-permute-start | bytes 202760 | tf_op jit(solution)/shard_map/ppermute | solution.py:19
  9.3 9.0 %collective-permute-start.1 = (f32[22,768]{1,0:T(8,128)S(1)}, f32[22,768]{1,0:T(8,128)S(1)}, u32[]{:S(2)}, u32[]{:S(2)}) collective-permute-start(f32[22,768]{1,0:T(8,128)S(1)} %get-tuple-element.254), channel_id=1, source_target_pairs={{8,0},{16,8},{24,16},{0,24},{9,1},{17,9},{25,17},{1,25},{10,2},{18... | collective-permute-start | bytes 202760 | tf_op jit(solution)/shard_map/ppermute | solution.py:20
  19.3 5.2 %collective-permute-start.2 = (f32[22,768]{1,0:T(8,128)S(1)}, f32[22,768]{1,0:T(8,128)S(1)}, u32[]{:S(2)}, u32[]{:S(2)}) collective-permute-start(f32[22,768]{1,0:T(8,128)S(1)} %get-tuple-element.251), channel_id=1, source_target_pairs={{0,1},{1,0},{2,3},{3,2},{4,5},{5,4},{6,7},{7,6},{8,9},{9,8},{10,11... | collective-permute-start | bytes 202760 | tf_op jit(solution)/shard_map/ppermute | solution.py:19
  21.7 4.4 %collective-permute-start.3 = (f32[22,768]{1,0:T(8,128)S(1)}, f32[22,768]{1,0:T(8,128)S(1)}, u32[]{:S(2)}, u32[]{:S(2)}) collective-permute-start(f32[22,768]{1,0:T(8,128)S(1)} %get-tuple-element.252), channel_id=1, source_target_pairs={{1,0},{0,1},{3,2},{2,3},{5,4},{4,5},{7,6},{6,7},{9,8},{8,9},{11,10... | collective-permute-start | bytes 202760 | tf_op jit(solution)/shard_map/ppermute | solution.py:20
  27.1 13.9 %collective-permute-start.4 = (f32[22,1536]{1,0:T(8,128)S(1)}, f32[22,1536]{1,0:T(8,128)S(1)}, u32[]{:S(2)}, u32[]{:S(2)}) collective-permute-start(f32[22,1536]{1,0:T(8,128)S(1)} %get-tuple-element.250), channel_id=1, source_target_pairs={{0,2},{2,4},{4,6},{6,0},{1,3},{3,5},{5,7},{7,1},{8,10},{10,12},{12... | collective-permute-start | bytes 405512 | tf_op jit(solution)/shard_map/ppermute | solution.py:19
  28.8 12.2 %collective-permute-start.5 = (f32[22,1536]{1,0:T(8,128)S(1)}, f32[22,1536]{1,0:T(8,128)S(1)}, u32[]{:S(2)}, u32[]{:S(2)}) collective-permute-start(f32[22,1536]{1,0:T(8,128)S(1)} %get-tuple-element.249), channel_id=1, source_target_pairs={{2,0},{4,2},{6,4},{0,6},{3,1},{5,3},{7,5},{1,7},{10,8},{12,10},{14... | collective-permute-start | bytes 405512 | tf_op jit(solution)/shard_map/ppermute | solution.py:20
where the time goes:
time: 44.7 us; the launch traced here: 44.3 us
  matrix products  11.1 us (25%)
  local copies, waits for them, and re-layouts  10.7 us (24%)
  starting transfers between devices  8.81 us (20%)
  other arithmetic  8.32 us (19%)
  waiting for transfers between devices  4.28 us (10%)
  loops' own time  0.57 us (1%)
  between operations  0.5 us (1%)
    dot_general x14, matrix products, add_group(): jnp.dot(portion, one_hot, precision=lax.Precision.HIGHEST, preferred_elem...  11.1 us
    ppermute x3, starting transfers between devices, padded_2(): before = lax.ppermute(last, axis, up)  4.57 us
    ppermute x3, starting transfers between devices, padded_2(): after = lax.ppermute(initial, axis, down)  4.24 us
    convert_element_type x3, other arithmetic, pick_blocks(): usable = (position < wanted).astype(jnp.float32)  3.79 us
    broadcast_in_dim x6, local copies, waits for them, and re-layouts, per_device(): jnp.broadcast_to(number[2 * section_index + side_index], (extent,))  3.78 us
    ppermute x3, waiting for transfers between devices, padded_2(): before = lax.ppermute(last, axis, up)  2.77 us
    gather x6, local copies, waits for them, and re-layouts, pick_blocks(): picked = jnp.take(holding, chosen, axis=1)  1.81 us
    slice x1, local copies, waits for them, and re-layouts, per_device(): number[2 * section_index + side_index]  1.54 us
  transfers between devices with their start and end apart: 6, of which 2 were waited for; matrix products, arithmetic and copies ran while one was open for 37% of the time, Pallas kernels for 0%

commit v1 on v0

v1 whole, which is shorter than its diff:
```python
import functools

import jax
import jax.numpy as jnp
from jax import lax
from jax.experimental import pallas as pl
from jax.experimental.pallas import tpu as pltpu
from jax.sharding import PartitionSpec as P

CELLS = 512
CAP_X = 6
CAP_Z = 6
CAP_Y = 12
LANES = 128
HALF = 256
GROUP = 8
GONE = 8 * CELLS
CLASSES = 3


def migrate_kernel(
    sizes,
    counts,
    lists,
    lists_row,
    fields_hbm,
    step_hbm,
    live_hbm,
    cell_hbm,
    out_ref,
    fields,
    step,
    live,
    cell,
    pool,
    offsets,
    acc,
    sent_x,
    sent_z,
    got_x,
    got_z,
    sent_y,
    got_y,
    load_sem,
    send_sem,
    recv_sem,
):
    field_count = fields_hbm.shape[0]
    rows = sent_x.shape[1]
    blocks = step.shape[0]

    me = {axis: lax.axis_index(axis) for axis in ("gx", "gy", "gz")}
    lower = {axis: {axis: lax.rem(me[axis] + sizes[axis] - 1, sizes[axis])} for axis in me}
    upper = {axis: {axis: lax.rem(me[axis] + 1, sizes[axis])} for axis in me}

    loads = [
        pltpu.make_async_copy(fields_hbm, fields, load_sem.at[0]),
        pltpu.make_async_copy(step_hbm, step, load_sem.at[1]),
        pltpu.make_async_copy(live_hbm, live, load_sem.at[2]),
        pltpu.make_async_copy(cell_hbm, cell, load_sem.at[3]),
    ]
    for load in loads:
        load.start()

    barrier = pltpu.get_barrier_semaphore()
    for axis in me:
        for neighbour in (lower[axis], upper[axis]):
            pl.semaphore_signal(
                barrier, inc=1, device_id=neighbour, device_id_type=pl.DeviceIdType.MESH
            )

    spans = (CAP_X, CAP_X, CAP_Z, CAP_Z, CAP_Y, CAP_Y)
    lane = lax.broadcasted_iota(jnp.int32, lists_row.shape, 1)
    limit = jnp.zeros(lists_row.shape, jnp.int32)
    away = jnp.zeros(lists_row.shape, jnp.float32)
    start = 0
    for k, span in enumerate(spans):
        here = lane >= start
        limit = jnp.where(here, counts[0, k] + start, limit)
        away = jnp.where(here, float(GONE if k < 4 else (k - 3) * CELLS), away)
        start += span
    away = jnp.where(lane < limit, away, 0.0)
    number = lax.broadcasted_iota(jnp.int32, (offsets.shape[0], lists_row.shape[1]), 0)
    named = jnp.where(lists_row[...] == number, away, 0.0)
    offsets[...] = jnp.broadcast_to(jnp.sum(named, axis=1, keepdims=True), offsets.shape)

    for load in loads:
        load.wait()

    first_row = lax.broadcasted_iota(jnp.int32, (8, LANES), 0)

    def own_block(e):
        v = fields[:, pl.ds(pl.multiple_of(e * LANES, LANES), LANES)]
        top = v[:8]
        pace = step[pl.ds(e, 1), :]
        top = top + jnp.where(first_row < 3, pace * pltpu.roll(top, 5, 0), 0.0)
        v = jnp.concatenate([top, v[8:]], axis=0)
        v = v * live[pl.ds(e, 1), :].astype(jnp.float32)
        where_to = cell[pl.ds(e, 1), :].astype(jnp.float32)
        return jnp.concatenate(
            [v, jnp.broadcast_to(where_to, (rows - field_count, LANES))], axis=0
        )

    def exchange(axis, index, sent, got, width):
        out = []
        for side, (target, other) in enumerate(((lower, 1), (upper, 0))):
            copy = pltpu.make_async_remote_copy(
                src_ref=sent.at[pl.ds(side * width, width)],
                dst_ref=got.at[pl.ds(other * width, width)],
                send_sem=send_sem.at[index + side],
                recv_sem=recv_sem.at[index + other],
                device_id=target[axis],
                device_id_type=pl.DeviceIdType.MESH,
            )
            copy.start()
            out.append(copy)
        return out

    def fill(sent, slot, span, first_entry, first_count):
        count = jnp.full((rows, LANES), counts[0, first_count + slot // span])
        block = pool[lists[0, first_entry + slot]]
        sent[slot] = jnp.where(count > slot % span, block, 0.0)

    def advance(g, carry):
        for i in range(GROUP):
            pool[g * GROUP + i] = own_block(g * GROUP + i)
        return carry

    lax.fori_loop(0, blocks // GROUP, advance, 0)
    for slot in range(2 * CAP_X):
        fill(sent_x, slot, CAP_X, 0, 0)
    pl.semaphore_wait(barrier, 6)
    copies_x = exchange("gx", 0, sent_x, got_x, CAP_X)

    code = lax.broadcasted_iota(jnp.int32, (HALF, LANES), 0).astype(jnp.float32)
    parts = CLASSES * CELLS // HALF

    def operands(v, cells):
        high = v.astype(jnp.bfloat16).astype(jnp.float32)
        both = jnp.concatenate([high, v - high], axis=0)
        part = jnp.floor(cells * (1.0 / HALF))
        inner = cells - part * HALF
        left = jnp.concatenate(
            [jnp.where(part == float(h), both, 0.0).astype(jnp.bfloat16) for h in range(parts)],
            axis=0,
        )
        right = jnp.where(code == inner, 1.0, 0.0).astype(jnp.bfloat16)
        return left, right

    def bin_group(pairs):
        left = jnp.concatenate([a for a, _ in pairs], axis=1)
        right = jnp.concatenate([b for _, b in pairs], axis=1)
        acc[...] += lax.dot_general(
            left, right, (((1,), (1,)), ((), ())), preferred_element_type=jnp.float32
        )

    acc[...] = jnp.zeros_like(acc)

    def bin_own(g, carry):
        pairs = []
        for i in range(GROUP):
            b = g * GROUP + i
            cells = pool[b, pl.ds(field_count, 1), :] + offsets[pl.ds(b, 1), :]
            pairs.append(operands(pool[b], cells))
        bin_group(pairs)
        return carry

    lax.fori_loop(0, blocks // GROUP, bin_own, 0)

    def bin_got(got, first, count, base):
        pairs = []
        for i in range(first, first + count):
            cells = got[i, pl.ds(field_count, 1), :] + offsets[pl.ds(base + i, 1), :]
            pairs.append(operands(got[i], cells))
        bin_group(pairs)

    for copy in copies_x:
        copy.wait_recv()
    for slot in range(2 * CAP_X):
        pool[blocks + slot] = got_x[slot]
    for slot in range(2 * CAP_Z):
        fill(sent_z, slot, CAP_Z, 2 * CAP_X, 2)
    copies_z = exchange("gz", 2, sent_z, got_z, CAP_Z)
    bin_got(got_x, 0, 2 * CAP_X, blocks)

    for side in (0, 1):
        pltpu.make_async_remote_copy(
            src_ref=sent_z.at[pl.ds((1 - side) * CAP_Z, CAP_Z)],
            dst_ref=got_z.at[pl.ds(side * CAP_Z, CAP_Z)],
            send_sem=send_sem.at[3 - side],
            recv_sem=recv_sem.at[2 + side],
            device_id=upper["gz"] if side == 0 else lower["gz"],
            device_id_type=pl.DeviceIdType.MESH,
        ).wait_recv()
        bin_got(got_z, side * CAP_Z, CAP_Z, blocks + 2 * CAP_X)

    def total(kind):
        halves = []
        for h in range(kind * CELLS // HALF, (kind + 1) * CELLS // HALF):
            top = 2 * rows * h
            halves.append(acc[pl.ds(top, rows), :] + acc[pl.ds(top + rows, rows), :])
        return jnp.concatenate(halves, axis=1)

    sent_y[0] = total(1)
    sent_y[1] = total(2)
    copies_y = exchange("gy", 4, sent_y, got_y, 1)
    kept = total(0)
    for copy in copies_y:
        copy.wait_recv()
    out_ref[...] = (kept + got_y[0] + got_y[1])[:field_count]
    for copy in copies_x + copies_z + copies_y:
        copy.wait_send()


def solution(mesh):
    sizes = {axis: mesh.shape[axis] for axis in ("gx", "gy", "gz")}

    def per_device(particle_fields, step_length, live_mask, dest_cell, block_counts, block_lists):
        field_count, particles = particle_fields.shape
        blocks = particles // LANES
        rows = (field_count + 1 + 7) // 8 * 8
        pool_blocks = blocks + 2 * CAP_X + 2 * CAP_Z
        by_block = [a.reshape(blocks, LANES) for a in (step_length, live_mask, dest_cell)]
        any_space = pl.BlockSpec(memory_space=pl.ANY)
        vmem = pl.BlockSpec(memory_space=pltpu.VMEM)
        smem = pl.BlockSpec(memory_space=pltpu.SMEM)
        f32 = jnp.float32
        return pl.pallas_call(
            functools.partial(migrate_kernel, sizes),
            out_shape=jax.ShapeDtypeStruct((field_count, CELLS), f32),
            in_specs=[smem, smem, vmem, any_space, any_space, any_space, any_space],
            out_specs=vmem,
            scratch_shapes=[
                pltpu.VMEM((field_count, particles), f32),
                pltpu.VMEM((blocks, LANES), f32),
                pltpu.VMEM((blocks, LANES), jnp.int32),
                pltpu.VMEM((blocks, LANES), jnp.int32),
                pltpu.VMEM((blocks + 2 * CAP_X, rows, LANES), f32),
                pltpu.VMEM((pool_blocks, LANES), f32),
                pltpu.VMEM((2 * rows * CLASSES * CELLS // HALF, HALF), f32),
                pltpu.VMEM((2 * CAP_X, rows, LANES), f32),
                pltpu.VMEM((2 * CAP_Z, rows, LANES), f32),
                pltpu.VMEM((2 * CAP_X, rows, LANES), f32),
                pltpu.VMEM((2 * CAP_Z, rows, LANES), f32),
                pltpu.VMEM((2, rows, CELLS), f32),
                pltpu.VMEM((2, rows, CELLS), f32),
                pltpu.SemaphoreType.DMA((4,)),
                pltpu.SemaphoreType.DMA((6,)),
                pltpu.SemaphoreType.DMA((6,)),
            ],
            compiler_params=pltpu.CompilerParams(collective_id=0, has_side_effects=True),
        )(block_counts, block_lists, block_lists, particle_fields, *by_block)

    placed = (
        P(None, ("gx", "gy", "gz")),
        P(("gx", "gy", "gz")),
        P(("gx", "gy", "gz")),
        P(("gx", "gy", "gz")),
        P(("gx", "gy", "gz"), None),
        P(("gx", "gy", "gz"), None),
    )
    return jax.shard_map(
        per_device,
        mesh=mesh,
        in_specs=placed,
        out_specs=P(None, ("gx", "gy", "gz")),
        check_vma=False,
    )
```

time: 44.7 us -> 22.4 us (0.50)
  Pallas kernels: 0 us -> 20.8 us
  matrix products: 11.1 us -> 0 us
  local copies, waits for them, and re-layouts: 10.7 us -> 1.42 us
  starting transfers between devices: 8.81 us -> 0 us
  other arithmetic: 8.32 us -> 0 us
  waiting for transfers between devices: 4.28 us -> 0 us
  loops' own time: 0.57 us -> 0 us
  between operations: 0.5 us -> 0.01 us
    pallas_call x0 -> x1, Pallas kernels: none -> 20.8 us  [per_device(): pl.pallas_call(functools.partial(migrate_kernel, sizes), out_shape=jax.Sh...]
    dot_general x14 -> x0, matrix products: 11.1 us -> none  [add_group(): jnp.dot(portion, one_hot, precision=lax.Precision.HIGHEST, preferred_elem...]
    ppermute x6 -> x0, starting transfers between devices: 8.81 us -> none  [the longest x3 4.57 us: padded_2(): before = lax.ppermute(last, axis, up)]
    ppermute x6 -> x0, waiting for transfers between devices: 4.28 us -> none  [the longest x3 2.77 us: padded_2(): before = lax.ppermute(last, axis, up)]
    broadcast_in_dim x8 -> x0, local copies, waits for them, and re-layouts: 3.93 us -> none  [the longest x6 3.78 us: per_device(): jnp.broadcast_to(number[2 * section_index + side_index], (extent,))]
    convert_element_type x5 -> x0, other arithmetic: 3.8 us -> none  [the longest x3 3.79 us: pick_blocks(): usable = (position < wanted).astype(jnp.float32)]
    slice x6 -> x0, local copies, waits for them, and re-layouts: 2.8 us -> none  [the longest x1 1.54 us: per_device(): number[2 * section_index + side_index]]
    gather x6 -> x0, local copies, waits for them, and re-layouts: 1.81 us -> none  [pick_blocks(): picked = jnp.take(holding, chosen, axis=1)]
  transfers between devices with their start and end apart: 6 -> 0, of which waited for: 2 -> 0; matrix products, arithmetic and copies ran while one was open for 37% -> 0% of each run, Pallas kernels for 0% -> 0%
where the time goes in v1:
time: 22.4 us; the launch traced here: 22.3 us
  Pallas kernels  20.8 us (93%)
  local copies, waits for them, and re-layouts  1.42 us (6%)
    pallas_call x1, Pallas kernels, per_device(): pl.pallas_call(functools.partial(migrate_kernel, sizes), out_shape=jax.Sh...  20.8 us
    unnamed x1, local copies, waits for them, and re-layouts  1.42 us

profile of v1, /device:TPU:0, one launch (start us, length us, event | category | flops | bytes accessed | tf_op | source)
XLA Modules:
  0.0 22.3 jit_solution(13979911836213762590)
XLA Ops:
  0.0 20.8 %shard_map.64 = f32[20,512]{1,0:T(8,128)} custom-call(s32[1,6]{1,0:T(1,128)} %counts.1, s32[1,48]{1,0:T(1,128)} %lists_row.1, s32[1,48]{1,0:T(1,128)} %lists_row.1, f32[20,8192]{1,0:T(8,128)} %fields_hbm.1, f32[64,128]{1,0:T(8,128)} %bitcast.3, s32[64,128]{1,0:T(8,128)} %bitcast.4, s32[64,128]{1,0:T(8,128)} %bitcast.5), custom_call_target="tpu_custom_call" | custom-call | tf_op jit(solution)/shard_map/pallas_call | solution.py:228
  20.8 1.4 %copy.8 = f32[20,512]{1,0:T(8,128)} copy(f32[20,512]{1,0:T(8,128)} %shard_map.64) | data formatting | bytes 81920

commit v2 on v1

--- a/solution.py
+++ b/solution.py
@@ -46,7 +46,9 @@
     recv_sem,
 ):
     field_count = fields_hbm.shape[0]
-    rows = sent_x.shape[1]
+    rows = pool.shape[1]
+    whole = field_count // 8 * 8
+    tail = field_count - whole
     blocks = step.shape[0]
 
     me = {axis: lax.axis_index(axis) for axis in ("gx", "gy", "gz")}
@@ -119,7 +121,20 @@
     def fill(sent, slot, span, first_entry, first_count):
         count = jnp.full((rows, LANES), counts[0, first_count + slot // span])
         block = pool[lists[0, first_entry + slot]]
-        sent[slot] = jnp.where(count > slot % span, block, 0.0)
+        block = jnp.where(count > slot % span, block, 0.0)
+        side, i = slot // span, slot % span
+        sent[side, pl.ds(i * whole, whole), :] = block[:whole]
+        tail_at = span * whole + i * tail
+        sent[side, pl.ds(tail_at, tail), :] = block[whole:field_count]
+        sent[side, pl.ds(span * field_count + i, 1), :] = block[field_count : field_count + 1]
+
+    def unpacked(got, slot, span):
+        side, i = slot // span, slot % span
+        body = got[side, pl.ds(i * whole, whole), :]
+        rest = got[side, pl.ds(span * whole + i * tail, tail), :]
+        cells = got[side, pl.ds(span * field_count + i, 1), :]
+        spare = jnp.broadcast_to(cells, (rows - field_count, LANES))
+        return jnp.concatenate([body, rest, spare], axis=0), cells
 
     def advance(g, carry):
         for i in range(GROUP):
@@ -130,18 +145,18 @@
     for slot in range(2 * CAP_X):
         fill(sent_x, slot, CAP_X, 0, 0)
     pl.semaphore_wait(barrier, 6)
-    copies_x = exchange("gx", 0, sent_x, got_x, CAP_X)
+    copies_x = exchange("gx", 0, sent_x, got_x, 1)
 
     code = lax.broadcasted_iota(jnp.int32, (HALF, LANES), 0).astype(jnp.float32)
     parts = CLASSES * CELLS // HALF
 
-    def operands(v, cells):
+    def operands(v, cells, wanted=tuple(range(parts))):
         high = v.astype(jnp.bfloat16).astype(jnp.float32)
         both = jnp.concatenate([high, v - high], axis=0)
         part = jnp.floor(cells * (1.0 / HALF))
         inner = cells - part * HALF
         left = jnp.concatenate(
-            [jnp.where(part == float(h), both, 0.0).astype(jnp.bfloat16) for h in range(parts)],
+            [jnp.where(part == float(h), both, 0.0).astype(jnp.bfloat16) for h in wanted],
             axis=0,
         )
         right = jnp.where(code == inner, 1.0, 0.0).astype(jnp.bfloat16)
@@ -165,49 +180,68 @@
         bin_group(pairs)
         return carry
 
-    lax.fori_loop(0, blocks // GROUP, bin_own, 0)
-
-    def bin_got(got, first, count, base):
+    early = 3 * (blocks // GROUP) // 8
+    lax.fori_loop(0, early, bin_own, 0)
+
+    def bin_got(got, side, width, base, wanted=tuple(range(parts))):
         pairs = []
-        for i in range(first, first + count):
-            cells = got[i, pl.ds(field_count, 1), :] + offsets[pl.ds(base + i, 1), :]
-            pairs.append(operands(got[i], cells))
-        bin_group(pairs)
+        for i in range(side * width, (side + 1) * width):
+            v, cells = unpacked(got, i, width)
+            pairs.append(operands(v, cells + offsets[pl.ds(base + i, 1), :], wanted))
+        left = jnp.concatenate([a for a, _ in pairs], axis=1)
+        right = jnp.concatenate([b for _, b in pairs], axis=1)
+        acc[pl.ds(2 * rows * wanted[0], 2 * rows * len(wanted)), :] += lax.dot_general(
+            left, right, (((1,), (1,)), ((), ())), preferred_element_type=jnp.float32
+        )
 
     for copy in copies_x:
         copy.wait_recv()
     for slot in range(2 * CAP_X):
-        pool[blocks + slot] = got_x[slot]
+        pool[blocks + slot] = unpacked(got_x, slot, CAP_X)[0]
     for slot in range(2 * CAP_Z):
         fill(sent_z, slot, CAP_Z, 2 * CAP_X, 2)
-    copies_z = exchange("gz", 2, sent_z, got_z, CAP_Z)
-    bin_got(got_x, 0, 2 * CAP_X, blocks)
-
-    for side in (0, 1):
+    copies_z = exchange("gz", 2, sent_z, got_z, 1)
+    lax.fori_loop(early, blocks // GROUP, bin_own, 0)
+    bin_got(got_x, 0, CAP_X, blocks)
+    bin_got(got_x, 1, CAP_X, blocks)
+
+    kept_parts = tuple(range(CELLS // HALF))
+    bound_parts = tuple(range(CELLS // HALF, parts))
+    late = blocks + 2 * CAP_X
+    for side in (1, 0):
         pltpu.make_async_remote_copy(
-            src_ref=sent_z.at[pl.ds((1 - side) * CAP_Z, CAP_Z)],
-            dst_ref=got_z.at[pl.ds(side * CAP_Z, CAP_Z)],
+            src_ref=sent_z.at[pl.ds(1 - side, 1)],
+            dst_ref=got_z.at[pl.ds(side, 1)],
             send_sem=send_sem.at[3 - side],
             recv_sem=recv_sem.at[2 + side],
             device_id=upper["gz"] if side == 0 else lower["gz"],
             device_id_type=pl.DeviceIdType.MESH,
         ).wait_recv()
-        bin_got(got_z, side * CAP_Z, CAP_Z, blocks + 2 * CAP_X)
-
-    def total(kind):
-        halves = []
-        for h in range(kind * CELLS // HALF, (kind + 1) * CELLS // HALF):
-            top = 2 * rows * h
-            halves.append(acc[pl.ds(top, rows), :] + acc[pl.ds(top + rows, rows), :])
-        return jnp.concatenate(halves, axis=1)
-
-    sent_y[0] = total(1)
-    sent_y[1] = total(2)
+        if side == 1:
+            bin_got(got_z, side, CAP_Z, late)
+        else:
+            bin_got(got_z, side, CAP_Z, late, bound_parts)
+
+    def bin_kept(base):
+        bin_got(got_z, 0, CAP_Z, base, kept_parts)
+
+    def halves(kind):
+        tops = [2 * rows * h for h in range(kind * CELLS // HALF, (kind + 1) * CELLS // HALF)]
+        return [
+            (acc[pl.ds(t, rows), :] + acc[pl.ds(t + rows, rows), :])[:field_count] for t in tops
+        ]
+
+    for side in (0, 1):
+        for i, half in enumerate(halves(side + 1)):
+            sent_y[side, pl.ds(i * field_count, field_count), :] = half
     copies_y = exchange("gy", 4, sent_y, got_y, 1)
-    kept = total(0)
+    bin_kept(late)
+    kept = halves(0)
     for copy in copies_y:
         copy.wait_recv()
-    out_ref[...] = (kept + got_y[0] + got_y[1])[:field_count]
+    for i, half in enumerate(kept):
+        part = pl.ds(i * field_count, field_count)
+        out_ref[:, pl.ds(i * HALF, HALF)] = half + got_y[0, part, :] + got_y[1, part, :]
     for copy in copies_x + copies_z + copies_y:
         copy.wait_send()
 
@@ -219,7 +253,12 @@
         field_count, particles = particle_fields.shape
         blocks = particles // LANES
         rows = (field_count + 1 + 7) // 8 * 8
+        sum_rows = (field_count * CELLS // HALF + 7) // 8 * 8
         pool_blocks = blocks + 2 * CAP_X + 2 * CAP_Z
+
+        def packed(span):
+            return (span * (field_count + 1) + 7) // 8 * 8
+
         by_block = [a.reshape(blocks, LANES) for a in (step_length, live_mask, dest_cell)]
         any_space = pl.BlockSpec(memory_space=pl.ANY)
         vmem = pl.BlockSpec(memory_space=pltpu.VMEM)
@@ -238,12 +277,12 @@
                 pltpu.VMEM((blocks + 2 * CAP_X, rows, LANES), f32),
                 pltpu.VMEM((pool_blocks, LANES), f32),
                 pltpu.VMEM((2 * rows * CLASSES * CELLS // HALF, HALF), f32),
-                pltpu.VMEM((2 * CAP_X, rows, LANES), f32),
-                pltpu.VMEM((2 * CAP_Z, rows, LANES), f32),
-                pltpu.VMEM((2 * CAP_X, rows, LANES), f32),
-                pltpu.VMEM((2 * CAP_Z, rows, LANES), f32),
-                pltpu.VMEM((2, rows, CELLS), f32),
-                pltpu.VMEM((2, rows, CELLS), f32),
+                pltpu.VMEM((2, packed(CAP_X), LANES), f32),
+                pltpu.VMEM((2, packed(CAP_Z), LANES), f32),
+                pltpu.VMEM((2, packed(CAP_X), LANES), f32),
+                pltpu.VMEM((2, packed(CAP_Z), LANES), f32),
+                pltpu.VMEM((2, sum_rows, HALF), f32),
+                pltpu.VMEM((2, sum_rows, HALF), f32),
                 pltpu.SemaphoreType.DMA((4,)),
                 pltpu.SemaphoreType.DMA((6,)),
                 pltpu.SemaphoreType.DMA((6,)),

time: 22.4 us -> 21.3 us (0.951)
  Pallas kernels: 20.8 us -> 19.7 us
    pallas_call x1, Pallas kernels: 20.8 us -> 19.7 us  [per_device(): pl.pallas_call(functools.partial(migrate_kernel, sizes), out_shape=jax.Sh...]
where the time goes in v2:
time: 21.3 us; the launch traced here: 21.1 us
  Pallas kernels  19.7 us (92%)
  local copies, waits for them, and re-layouts  1.42 us (7%)
    pallas_call x1, Pallas kernels, per_device(): pl.pallas_call(functools.partial(migrate_kernel, sizes), out_shape=jax.Sh...  19.7 us
    unnamed x1, local copies, waits for them, and re-layouts  1.42 us

profile of v2, /device:TPU:0, one launch (start us, length us, event | category | flops | bytes accessed | tf_op | source)
XLA Modules:
  0.0 21.1 jit_solution(18296378650798866207)
XLA Ops:
  0.0 19.7 %shard_map.64 = f32[20,512]{1,0:T(8,128)} custom-call(s32[1,6]{1,0:T(1,128)} %counts.1, s32[1,48]{1,0:T(1,128)} %lists_row.1, s32[1,48]{1,0:T(1,128)} %lists_row.1, f32[20,8192]{1,0:T(8,128)} %fields_hbm.1, f32[64,128]{1,0:T(8,128)} %bitcast.3, s32[64,128]{1,0:T(8,128)} %bitcast.4, s32[64,128]{1,0:T(8,128)} %bitcast.5), custom_call_target="tpu_custom_call" | custom-call | tf_op jit(solution)/shard_map/pallas_call | solution.py:267
  19.7 1.4 %copy.8 = f32[20,512]{1,0:T(8,128)} copy(f32[20,512]{1,0:T(8,128)} %shard_map.64) | data formatting | bytes 81920
